TPU v7x, 512 devices: a whole 4x8x8 slice. The times are simulated.
512 devices in a mesh: seq: 16 (over y, core), exp: 32 (over x, z).
Axes of the slice: x: 4, y: 8, z: 8, core: 2. Of those that a mesh axis runs over, the one named last changes fastest.
Arguments:
- tokens: bfloat16 [65536, 1280], P(('seq', 'exp')), may hold values from -64 to 64
- slot_keys: bfloat16 [1280, 32], P(None, 'exp'), may hold values from -3 to 3
- w_in: bfloat16 [32, 5120, 1280], P('exp', 'seq'), may hold values from -0.15625 to 0.15625
- w_out: bfloat16 [32, 5120, 1280], P('exp', 'seq'), may hold values from -0.078125 to 0.078125
- cotangent: bfloat16 [65536, 1280], P(('seq', 'exp')), may hold values from -6 to 6
Outputs:
- layer_out: bfloat16 [65536, 1280], P(('seq', 'exp'))
- tokens_grad: bfloat16 [65536, 1280], P(('seq', 'exp'))
- keys_grad: float32 [1280, 32], P(None, 'exp')
- w_in_grad: bfloat16 [32, 5120, 1280], P('exp', 'seq')
- w_out_grad: bfloat16 [32, 5120, 1280], P('exp', 'seq')
All inputs are finite; a program needn't handle non-finite values.
Results may differ from a plain program's by a relative error of at most 0.03.
Values may be sent and summed in bfloat16 or wider, within the bound.
A program may use at most 64 MiB of HBM per device.

v0:
```python
import jax
import jax.numpy as jnp
from jax import lax
from jax.sharding import Mesh
from jax.sharding import PartitionSpec as P

EXP = ("exp_0", "exp_1")
SEQ = ("seq_0", "seq_1")
SEQ_EXP = ("seq_0", "seq_1", "exp_0", "exp_1")
tanh_coeff = 0.7978845608028654
cubic_coeff = 0.044715


def cut_along(value, dim, size):
    before, after = (value.shape[:dim], value.shape[dim + 1 :])
    return jnp.moveaxis(value.reshape(*before, size, -1, *after), dim, 0)


def sent_and_summed(value, axis, dim):
    tiles = cut_along(value, dim, lax.axis_size(axis))
    arrived = lax.all_to_all(tiles, axis, split_axis=0, concat_axis=0, tiled=True)
    return arrived.sum(axis=0)


def sent_to_all(value, axis):
    copies = jnp.broadcast_to(value, (lax.axis_size(axis), *value.shape))
    return lax.all_to_all(copies, axis, split_axis=0, concat_axis=0, tiled=True)


def taken_together(value, axis):
    return sent_to_all(value, axis).sum(axis=0)


def laid_out(tiles, dim):
    tiles = jnp.moveaxis(tiles, 0, dim)
    lengths = tiles.shape
    return tiles.reshape(*lengths[:dim], lengths[dim] * lengths[dim + 1], *lengths[dim + 2 :])


def gathered_copies(value, axis, dim):
    return laid_out(sent_to_all(value, axis), dim)


def collected_together(value, axis):
    leaves = jax.tree.leaves(value)
    sequence = sorted(range(len(leaves)), key=lambda k: -leaves[k].size)
    width = (1, *leaves[sequence[0]].shape)[-1]
    lines = [
        jnp.pad(leaves[k].reshape(-1), (0, -leaves[k].size % width)).reshape(-1, width)
        for k in sequence
    ]
    both, at, found = (lax.all_gather(jnp.concatenate(lines), axis), 0, {})
    for k, line in zip(sequence, lines):
        slab = both[:, at : at + len(line)].reshape(len(both), -1)
        found[k] = slab[:, : leaves[k].size].reshape(-1, *leaves[k].shape)
        at += len(line)
    numbers = iter(range(len(leaves)))
    return jax.tree.map(lambda _: found[next(numbers)], value)


def merged_by_axis(value, axes, combine):
    for axis in axes:
        pieces = collected_together(value, axis)
        value = jax.tree.map(lambda part: part[0], pieces)
        for k in range(1, lax.axis_size(axis)):
            value = combine(value, jax.tree.map(lambda part: part[k], pieces))
    return value


def by_axis(value, axes):
    for axis in axes:
        value = lax.psum(value, axis)
    return value


def gelu_value(values):
    return (
        0.5
        * values
        * (1.0 + jnp.tanh(tanh_coeff * (values + cubic_coeff * values * values * values)))
    )


def gelu_slope(values):
    tanh_part = jnp.tanh(tanh_coeff * (values + cubic_coeff * values * values * values))
    return 0.5 * (1.0 + tanh_part) + 0.5 * values * (1.0 - tanh_part * tanh_part) * tanh_coeff * (
        1.0 + 3.0 * cubic_coeff * values * values
    )


def join_stats(earlier, later):
    top_score = jnp.maximum(earlier[0], later[0])
    summed = earlier[1] * jnp.exp(earlier[0] - top_score) + later[1] * jnp.exp(later[0] - top_score)
    return (top_score, summed)


def rows_of(weights, row_data):

    def make_rows(first_row, row_count):
        return jnp.dot(weights, row_data, preferred_element_type=jnp.float32)

    return make_rows


def rows_paired(first_weights, first_data, second_weights, second_data):

    def make_rows(first_row, row_count):
        return jnp.concatenate(
            [
                jnp.dot(first_weights, first_data, preferred_element_type=jnp.float32),
                jnp.dot(second_weights, second_data, preferred_element_type=jnp.float32),
            ],
            axis=1,
        )

    return make_rows


def to_owners(make_rows, local_experts):
    owned_rows = sent_and_summed(
        make_rows(jnp.int32(0), local_experts * lax.axis_size(EXP)), EXP, 0
    )
    result = taken_together(owned_rows, SEQ)
    return result


def to_tokens(partial_value):
    summed = taken_together(partial_value, SEQ)
    return gathered_copies(summed.astype(jnp.bfloat16), EXP, 0)


def local(tokens, slot_keys, w_in, w_out, cotangent):
    local_experts = w_in.shape[0]
    width = tokens.shape[1]
    keys_all = gathered_copies(slot_keys, EXP, 1)
    logits = lax.dot_general(
        keys_all, tokens, (((0,), (1,)), ((), ())), preferred_element_type=jnp.float32
    )
    local_peak = jnp.max(logits, axis=1)
    local_total = jnp.sum(jnp.exp(logits - local_peak[:, None]), axis=1)
    slot_peak, slot_total = merged_by_axis((local_peak, local_total), SEQ_EXP, join_stats)
    exp_terms = jnp.exp(logits - slot_peak[:, None])
    disp_prob = exp_terms / slot_total[:, None]
    dispatch = disp_prob.astype(jnp.bfloat16)
    row_peak = jnp.max(logits, axis=0, keepdims=True)
    row_terms = jnp.exp(logits - row_peak)
    comb_prob = row_terms / jnp.sum(row_terms, axis=0, keepdims=True)
    combine = comb_prob.astype(jnp.bfloat16)
    both_rows = to_owners(rows_paired(dispatch, tokens, combine, cotangent), local_experts).astype(
        jnp.bfloat16
    )
    slot_in = both_rows[:, :width]
    early_grad = both_rows[:, width:]
    pre_act = jnp.einsum("efd,ed->ef", w_in, slot_in, preferred_element_type=jnp.float32)
    activation = gelu_value(pre_act).astype(jnp.bfloat16)
    slot_out = to_tokens(
        jnp.einsum("ef,efd->ed", activation, w_out, preferred_element_type=jnp.float32)
    )
    layer_out = lax.dot_general(
        combine, slot_out, (((0,), (0,)), ((), ())), preferred_element_type=jnp.float32
    ).astype(jnp.bfloat16)
    comb_grad = lax.dot_general(
        slot_out, cotangent, (((1,), (1,)), ((), ())), preferred_element_type=jnp.float32
    )
    act_grad = jnp.einsum("efd,ed->ef", w_out, early_grad, preferred_element_type=jnp.float32)
    w_out_grad = (
        activation.astype(jnp.float32)[:, :, None] * early_grad.astype(jnp.float32)[:, None, :]
    ).astype(jnp.bfloat16)
    pre_grad = (act_grad * gelu_slope(pre_act)).astype(jnp.bfloat16)
    w_in_grad = (
        pre_grad.astype(jnp.float32)[:, :, None] * slot_in.astype(jnp.float32)[:, None, :]
    ).astype(jnp.bfloat16)
    slot_in_grad = to_tokens(
        jnp.einsum("ef,efd->ed", pre_grad, w_in, preferred_element_type=jnp.float32)
    )
    disp_grad = lax.dot_general(
        slot_in_grad, tokens, (((1,), (1,)), ((), ())), preferred_element_type=jnp.float32
    )
    correction = by_axis(jnp.sum(disp_prob * disp_grad, axis=1), SEQ_EXP)
    comb_mean = jnp.sum(comb_prob * comb_grad, axis=0, keepdims=True)
    logit_grad = (
        comb_prob * (comb_grad - comb_mean) + disp_prob * (disp_grad - correction[:, None])
    ).astype(jnp.bfloat16)
    tokens_grad = (
        lax.dot_general(
            dispatch, slot_in_grad, (((0,), (0,)), ((), ())), preferred_element_type=jnp.float32
        )
        + lax.dot_general(
            logit_grad, keys_all, (((0,), (1,)), ((), ())), preferred_element_type=jnp.float32
        )
    ).astype(jnp.bfloat16)
    keys_rows = to_owners(rows_of(logit_grad, tokens), local_experts)
    keys_grad = keys_rows.T
    return (layer_out, tokens_grad, keys_grad, w_in_grad, w_out_grad)


def solution(mesh):
    finer = Mesh(mesh.devices.reshape(8, 2, 4, 8), ("seq_0", "seq_1", "exp_0", "exp_1"))
    placed = (
        P(SEQ_EXP, None),
        P(None, EXP),
        P(EXP, SEQ, None),
        P(EXP, SEQ, None),
        P(SEQ_EXP, None),
    )
    return jax.shard_map(
        local,
        mesh=finer,
        in_specs=placed,
        out_specs=(
            P(SEQ_EXP, None),
            P(SEQ_EXP, None),
            P(None, EXP),
            P(EXP, SEQ, None),
            P(EXP, SEQ, None),
        ),
        check_vma=False,
    )
```

profile of v0, /device:TPU:1, one launch (start us, length us, event | category | flops | bytes accessed | tf_op | source)
XLA Modules:
  0.0 225.8 jit_solution(24418915979443625)
XLA Ops:
  0.7 0.8 reduce.6
  2.1 1.1 reduce.19
  3.2 22.6 %all_to_all.45 = bf16[32,2,640]{2,1,0:T(2,128)(2,1)S(1)} all-to-all(bf16[32,2,640]{2,1,0:T(2,128)(2,1)S(1)} %reshape.1141), channel_id=1, replica_groups=mesh['seq_0'=8,'seq_1'=2,'exp_0'=4,'exp_1'=8] {'exp_0','exp_1'}, dimensions={0} | all-to-all | bytes 163840 | tf_op jit(solution)/shard_map/all_to_all | solution.py:27
  26.4 13.3 %all-gather.4 = f32[8,2,32]{2,1,0:T(2,128)S(1)} all-gather(f32[1,2,32]{2,1,0:T(2,128)S(1)} %maximum_bitcast_fusion.1), channel_id=2, replica_groups=mesh['seq_0'=8,'seq_1'=2,'exp_0'=4,'exp_1'=8] {'seq_0'}, dimensions={0}, use_global_device_ids=true | all-gather | bytes 2304 | tf_op jit(solution)/shard_map/all_gather | solution.py:52
  39.8 7.0 %all-gather.5 = f32[2,2,32]{2,1,0:T(2,128)S(1)} all-gather(f32[1,2,32]{2,1,0:T(2,128)S(1)} %maximum_bitcast_fusion.2), channel_id=3, replica_groups=mesh['seq_0'=8,'seq_1'=2,'exp_0'=4,'exp_1'=8] {'seq_1'}, dimensions={0}, use_global_device_ids=true | all-gather | bytes 768 | tf_op jit(solution)/shard_map/all_gather | solution.py:52
  46.8 6.1 %all-gather.6 = f32[4,2,32]{2,1,0:T(2,128)S(1)} all-gather(f32[1,2,32]{2,1,0:T(2,128)S(1)} %maximum_bitcast_fusion.3), channel_id=4, replica_groups=mesh['seq_0'=8,'seq_1'=2,'exp_0'=4,'exp_1'=8] {'exp_0'}, dimensions={0}, use_global_device_ids=true | all-gather | bytes 1280 | tf_op jit(solution)/shard_map/all_gather | solution.py:52
  53.0 10.5 %all-gather.7 = f32[8,2,32]{2,1,0:T(2,128)S(1)} all-gather(f32[1,2,32]{2,1,0:T(2,128)S(1)} %maximum_bitcast_fusion.4), channel_id=5, replica_groups=mesh['seq_0'=8,'seq_1'=2,'exp_0'=4,'exp_1'=8] {'exp_1'}, dimensions={0}, use_global_device_ids=true | all-gather | bytes 2304 | tf_op jit(solution)/shard_map/all_gather | solution.py:52
  64.3 14.2 %all_to_all.46 = f32[32,1,2560]{2,1,0:T(1,128)S(1)} all-to-all(f32[32,1,2560]{2,1,0:T(1,128)S(1)} %copy.17), channel_id=1, replica_groups=mesh['seq_0'=8,'seq_1'=2,'exp_0'=4,'exp_1'=8] {'exp_0','exp_1'}, dimensions={0} | all-to-all | bytes 655360 | tf_op jit(solution)/shard_map/all_to_all | solution.py:21
  78.8 21.2 %all_to_all.47 = f32[16,1,2560]{2,1,0:T(1,128)S(1)} all-to-all(f32[16,1,2560]{2,1,0:T(1,128)S(1)} %broadcast_in_dim.15), channel_id=1, replica_groups=mesh['seq_0'=8,'seq_1'=2,'exp_0'=4,'exp_1'=8] {'seq_0','seq_1'}, dimensions={0} | all-to-all | bytes 327680 | tf_op jit(solution)/shard_map/all_to_all | solution.py:27
  101.2 0.7 broadcast_in_dim.36
  101.8 3.4 %all-to-all-start.5 = ((f32[16,1,1280]{2,1,0:T(1,128)}), f32[16,1,1280]{2,1,0:T(1,128)S(1)}, u32[]{:S(2)}, u32[]{:S(2)}) async-start(f32[16,1,1280]{2,1,0:T(1,128)} %broadcast_in_dim.36), calls=%async_computation.5 | async-start | bytes 163840 | tf_op jit(solution)/shard_map/all_to_all | solution.py:27
  105.5 7.4 %all-to-all-done.5 = f32[16,1,1280]{2,1,0:T(1,128)S(1)} async-done(((f32[16,1,1280]{2,1,0:T(1,128)}), f32[16,1,1280]{2,1,0:T(1,128)S(1)}, u32[]{:S(2)}, u32[]{:S(2)}) %all-to-all-start.5) | async-done | bytes 81952 | tf_op jit(solution)/shard_map/all_to_all | solution.py:27
  113.6 3.4 %all-to-all-start.3 = ((f32[16,1,1280]{2,1,0:T(1,128)}), f32[16,1,1280]{2,1,0:T(1,128)S(1)}, u32[]{:S(2)}, u32[]{:S(2)}) async-start(f32[16,1,1280]{2,1,0:T(1,128)} %broadcast_in_dim.16), calls=%async_computation.3 | async-start | bytes 163840 | tf_op jit(solution)/shard_map/all_to_all | solution.py:27
  117.3 1.1 reduce.21
  119.0 6.2 %all-to-all-done.3 = f32[16,1,1280]{2,1,0:T(1,128)S(1)} async-done(((f32[16,1,1280]{2,1,0:T(1,128)}), f32[16,1,1280]{2,1,0:T(1,128)S(1)}, u32[]{:S(2)}, u32[]{:S(2)}) %all-to-all-start.3) | async-done | bytes 81952 | tf_op jit(solution)/shard_map/all_to_all | solution.py:27
  125.2 4.8 %all-to-all-start.6 = ((bf16[32,2,640]{2,1,0:T(2,128)(2,1)}), bf16[32,2,640]{2,1,0:T(2,128)(2,1)S(1)}, u32[]{:S(2)}, u32[]{:S(2)}) async-start(bf16[32,2,640]{2,1,0:T(2,128)(2,1)} %reshape.1145), calls=%async_computation.6 | async-start | bytes 163840 | tf_op jit(solution)/shard_map/all_to_all | solution.py:27
  130.0 1.4 multiply_convert_fusion
  131.6 1.1 reduce.20
  133.3 5.6 %all-to-all-done.6 = bf16[32,2,640]{2,1,0:T(2,128)(2,1)S(1)} async-done(((bf16[32,2,640]{2,1,0:T(2,128)(2,1)}), bf16[32,2,640]{2,1,0:T(2,128)(2,1)S(1)}, u32[]{:S(2)}, u32[]{:S(2)}) %all-to-all-start.6) | async-done | bytes 81952 | tf_op jit(solution)/shard_map/all_to_all | solution.py:27
  138.9 3.9 %all-to-all-start.4 = ((bf16[32,2,640]{2,1,0:T(2,128)(2,1)}), bf16[32,2,640]{2,1,0:T(2,128)(2,1)S(1)}, u32[]{:S(2)}, u32[]{:S(2)}) async-start(bf16[32,2,640]{2,1,0:T(2,128)(2,1)} %reshape.1143), calls=%async_computation.4 | async-start | bytes 163840 | tf_op jit(solution)/shard_map/all_to_all | solution.py:27
  143.0 8.8 %all-to-all-done.4 = bf16[32,2,640]{2,1,0:T(2,128)(2,1)S(1)} async-done(((bf16[32,2,640]{2,1,0:T(2,128)(2,1)}), bf16[32,2,640]{2,1,0:T(2,128)(2,1)S(1)}, u32[]{:S(2)}, u32[]{:S(2)}) %all-to-all-start.4) | async-done | bytes 81952 | tf_op jit(solution)/shard_map/all_to_all | solution.py:27
  152.1 10.9 %psum.28 = f32[32]{0:T(128)S(1)} all-reduce(f32[32]{0:T(128)S(1)} %get-tuple-element.6), channel_id=1, replica_groups=mesh['seq_0'=8,'seq_1'=2,'exp_0'=4,'exp_1'=8] {'seq_0'}, use_global_device_ids=true, to_apply=%region_10.11 | all-reduce | flops 32 | bytes 256 | tf_op jit(solution)/shard_map/psum | solution.py:72
  163.0 8.6 %psum.29 = f32[32]{0:T(128)S(1)} all-reduce(f32[32]{0:T(128)S(1)} %psum.28), channel_id=1, replica_groups=mesh['seq_0'=8,'seq_1'=2,'exp_0'=4,'exp_1'=8] {'seq_1'}, use_global_device_ids=true, to_apply=%region_11.12 | all-reduce | flops 32 | bytes 256 | tf_op jit(solution)/shard_map/psum | solution.py:72
  171.6 6.8 %psum.30 = f32[32]{0:T(128)S(1)} all-reduce(f32[32]{0:T(128)S(1)} %psum.29), channel_id=1, replica_groups=mesh['seq_0'=8,'seq_1'=2,'exp_0'=4,'exp_1'=8] {'exp_0'}, use_global_device_ids=true, to_apply=%region_12.13 | all-reduce | flops 32 | bytes 256 | tf_op jit(solution)/shard_map/psum | solution.py:72
  178.4 11.3 %psum.31 = f32[32]{0:T(128)S(1)} all-reduce(f32[32]{0:T(128)S(1)} %psum.30), channel_id=1, replica_groups=mesh['seq_0'=8,'seq_1'=2,'exp_0'=4,'exp_1'=8] {'exp_1'}, use_global_device_ids=true, to_apply=%region_13.14 | all-reduce | flops 32 | bytes 256 | tf_op jit(solution)/shard_map/psum | solution.py:72
  189.9 0.8 copy.21
  190.8 4.4 %all-to-all-start.7 = ((f32[32,1,1280]{2,1,0:T(1,128)}), f32[32,1,1280]{2,1,0:T(1,128)S(1)}, u32[]{:S(2)}, u32[]{:S(2)}) async-start(f32[32,1,1280]{2,1,0:T(1,128)} %copy.21), calls=%async_computation.7 | async-start | bytes 327680 | tf_op jit(solution)/shard_map/all_to_all | solution.py:21
  195.5 1.1 fusion
  196.6 7.8 %all-to-all-done.7 = f32[32,1,1280]{2,1,0:T(1,128)S(1)} async-done(((f32[32,1,1280]{2,1,0:T(1,128)}), f32[32,1,1280]{2,1,0:T(1,128)S(1)}, u32[]{:S(2)}, u32[]{:S(2)}) %all-to-all-start.7) | async-done | bytes 163872 | tf_op jit(solution)/shard_map/all_to_all | solution.py:21
  205.2 11.8 %all-to-all-start.8 = ((f32[16,1,1280]{2,1,0:T(1,128)}), f32[16,1,1280]{2,1,0:T(1,128)S(1)}, u32[]{:S(2)}, u32[]{:S(2)}) async-start(f32[16,1,1280]{2,1,0:T(1,128)} %broadcast_in_dim.38), calls=%async_computation.8 | async-start | bytes 163840 | tf_op jit(solution)/shard_map/all_to_all | solution.py:27
  217.0 1.0 convolution_convert_fusion
  218.0 7.1 %all-to-all-done.8 = f32[16,1,1280]{2,1,0:T(1,128)S(1)} async-done(((f32[16,1,1280]{2,1,0:T(1,128)}), f32[16,1,1280]{2,1,0:T(1,128)S(1)}, u32[]{:S(2)}, u32[]{:S(2)}) %all-to-all-start.8) | async-done | bytes 81952 | tf_op jit(solution)/shard_map/all_to_all | solution.py:27
  (57 shorter events, 8.6 us)
Async XLA Ops:
  0.6 99.9 %copy-start = (bf16[1,320,1280]{2,1,0:T(8,128)(2,1)S(1)}, bf16[1,320,1280]{2,1,0:T(8,128)(2,1)}, u32[]{:S(2)}) copy-start(bf16[1,320,1280]{2,1,0:T(8,128)(2,1)} %param.7) | copy-start | bytes 2457604
  0.6 25.2 %copy-start.1 = (bf16[128,1280]{1,0:T(8,128)(2,1)S(1)}, bf16[128,1280]{1,0:T(8,128)(2,1)}, u32[]{:S(2)}) copy-start(bf16[128,1280]{1,0:T(8,128)(2,1)} %param.5) | copy-start | bytes 983044
  3.2 60.6 %copy-start.3 = (bf16[128,1280]{1,0:T(8,128)(2,1)S(1)}, bf16[128,1280]{1,0:T(8,128)(2,1)}, u32[]{:S(2)}) copy-start(bf16[128,1280]{1,0:T(8,128)(2,1)} %param.9) | copy-start | bytes 983044
  64.3 35.9 %copy-start.2 = (bf16[1,320,1280]{2,1,0:T(8,128)(2,1)S(1)}, bf16[1,320,1280]{2,1,0:T(8,128)(2,1)}, u32[]{:S(2)}) copy-start(bf16[1,320,1280]{2,1,0:T(8,128)(2,1)} %param.8) | copy-start | bytes 2457604
  101.8 11.1 %all-to-all-start.5 = ((f32[16,1,1280]{2,1,0:T(1,128)}), f32[16,1,1280]{2,1,0:T(1,128)S(1)}, u32[]{:S(2)}, u32[]{:S(2)}) async-start(f32[16,1,1280]{2,1,0:T(1,128)} %broadcast_in_dim.36), calls=%async_computation.5 | async-start | bytes 163840 | tf_op jit(solution)/shard_map/all_to_all | solution.py:27
  113.6 11.6 %all-to-all-start.3 = ((f32[16,1,1280]{2,1,0:T(1,128)}), f32[16,1,1280]{2,1,0:T(1,128)S(1)}, u32[]{:S(2)}, u32[]{:S(2)}) async-start(f32[16,1,1280]{2,1,0:T(1,128)} %broadcast_in_dim.16), calls=%async_computation.3 | async-start | bytes 163840 | tf_op jit(solution)/shard_map/all_to_all | solution.py:27
  125.2 13.8 %all-to-all-start.6 = ((bf16[32,2,640]{2,1,0:T(2,128)(2,1)}), bf16[32,2,640]{2,1,0:T(2,128)(2,1)S(1)}, u32[]{:S(2)}, u32[]{:S(2)}) async-start(bf16[32,2,640]{2,1,0:T(2,128)(2,1)} %reshape.1145), calls=%async_computation.6 | async-start | bytes 163840 | tf_op jit(solution)/shard_map/all_to_all | solution.py:27
  138.9 12.9 %all-to-all-start.4 = ((bf16[32,2,640]{2,1,0:T(2,128)(2,1)}), bf16[32,2,640]{2,1,0:T(2,128)(2,1)S(1)}, u32[]{:S(2)}, u32[]{:S(2)}) async-start(bf16[32,2,640]{2,1,0:T(2,128)(2,1)} %reshape.1143), calls=%async_computation.4 | async-start | bytes 163840 | tf_op jit(solution)/shard_map/all_to_all | solution.py:27
  190.8 13.6 %all-to-all-start.7 = ((f32[32,1,1280]{2,1,0:T(1,128)}), f32[32,1,1280]{2,1,0:T(1,128)S(1)}, u32[]{:S(2)}, u32[]{:S(2)}) async-start(f32[32,1,1280]{2,1,0:T(1,128)} %copy.21), calls=%async_computation.7 | async-start | bytes 327680 | tf_op jit(solution)/shard_map/all_to_all | solution.py:21
  205.2 19.9 %all-to-all-start.8 = ((f32[16,1,1280]{2,1,0:T(1,128)}), f32[16,1,1280]{2,1,0:T(1,128)S(1)}, u32[]{:S(2)}, u32[]{:S(2)}) async-start(f32[16,1,1280]{2,1,0:T(1,128)} %broadcast_in_dim.38), calls=%async_computation.8 | async-start | bytes 163840 | tf_op jit(solution)/shard_map/all_to_all | solution.py:27
where the time goes:
time: 227 us; the launch traced here: 226 us
  blocking collectives  133 us (59%)
  waiting for transfers between devices  42.9 us (19%)
  starting transfers between devices  31.7 us (14%)
  other arithmetic  6.5 us (3%)
  local copies, waits for them, and re-layouts  6.29 us (3%)
  matrix products  4.99 us (2%)
    all_to_all x2, blocking collectives, sent_to_all(): return lax.all_to_all(copies, axis, split_axis=0, concat_axis=0, tiled=True)  43.8 us
    psum x4, blocking collectives, by_axis(): value = lax.psum(value, axis)  37.6 us
    all_gather x4, blocking collectives, collected_together(): both, at, found = (lax.all_gather(jnp.concatenate(lines), axis), 0, {})  37 us
    all_to_all x5, waiting for transfers between devices, sent_to_all(): return lax.all_to_all(copies, axis, split_axis=0, concat_axis=0, tiled=True)  35.1 us
    all_to_all x5, starting transfers between devices, sent_to_all(): return lax.all_to_all(copies, axis, split_axis=0, concat_axis=0, tiled=True)  27.3 us
    all_to_all x1, blocking collectives, sent_and_summed(): lax.all_to_all(tiles, axis, split_axis=0, concat_axis=0, tiled=True)  14.2 us
    all_to_all x1, waiting for transfers between devices, sent_and_summed(): lax.all_to_all(tiles, axis, split_axis=0, concat_axis=0, tiled=True)  7.81 us
  transfers between devices with their start and end apart: 6, of which 6 were waited for; matrix products, arithmetic and copies ran while one was open for 4% of the time, Pallas kernels for 0%

commit v1 on v0

--- a/solution.py
+++ b/solution.py
@@ -69,7 +69,7 @@
 
 def by_axis(value, axes):
     for axis in axes:
-        value = lax.psum(value, axis)
+        value = jnp.sum(lax.all_gather(value, axis), axis=0)
     return value
 
 

time: 227 us -> 234 us (1.031)
  blocking collectives: 133 us -> 121 us
  local copies, waits for them, and re-layouts: 6.29 us -> 13.4 us
  starting transfers between devices: 31.7 us -> 36.5 us
  waiting for transfers between devices: 42.9 us -> 46.5 us
  between operations: 0.89 us -> 3.51 us
    unnamed x0 -> x4, blocking collectives: none -> 40.3 us
    psum x4 -> x0, blocking collectives: 37.6 us -> none  [by_axis(): value = lax.psum(value, axis)]
    all_to_all x1 -> x0, blocking collectives: 14.2 us -> none  [sent_and_summed(): lax.all_to_all(tiles, axis, split_axis=0, concat_axis=0, tiled=True)]
    all_to_all x1 -> x2, waiting for transfers between devices: 7.81 us -> 17.7 us  [sent_and_summed(): lax.all_to_all(tiles, axis, split_axis=0, concat_axis=0, tiled=True)]
    all_to_all x5, waiting for transfers between devices: 35.1 us -> 28.8 us  [sent_to_all(): return lax.all_to_all(copies, axis, split_axis=0, concat_axis=0, tiled=True)]
    unnamed x16 -> x28, local copies, waits for them, and re-layouts: 2.16 us -> 8.19 us
    all_to_all x1 -> x2, starting transfers between devices: 4.36 us -> 8.89 us  [sent_and_summed(): lax.all_to_all(tiles, axis, split_axis=0, concat_axis=0, tiled=True)]
  transfers between devices with their start and end apart: 6 -> 7, of which waited for: 6 -> 6; matrix products, arithmetic and copies ran while one was open for 4% -> 6% of each run, Pallas kernels for 0% -> 0%
where the time goes in v1:
time: 234 us; the launch traced here: 233 us
  blocking collectives  121 us (52%)
  waiting for transfers between devices  46.5 us (20%)
  starting transfers between devices  36.5 us (16%)
  local copies, waits for them, and re-layouts  13.4 us (6%)
  other arithmetic  6.59 us (3%)
  matrix products  4.99 us (2%)
  between operations  3.51 us (2%)
    all_to_all x2, blocking collectives, sent_to_all(): return lax.all_to_all(copies, axis, split_axis=0, concat_axis=0, tiled=True)  43.8 us
    unnamed x4, blocking collectives  40.3 us
    all_gather x4, blocking collectives, collected_together(): both, at, found = (lax.all_gather(jnp.concatenate(lines), axis), 0, {})  37 us
    all_to_all x5, waiting for transfers between devices, sent_to_all(): return lax.all_to_all(copies, axis, split_axis=0, concat_axis=0, tiled=True)  28.8 us
    all_to_all x5, starting transfers between devices, sent_to_all(): return lax.all_to_all(copies, axis, split_axis=0, concat_axis=0, tiled=True)  27.6 us
    all_to_all x2, waiting for transfers between devices, sent_and_summed(): lax.all_to_all(tiles, axis, split_axis=0, concat_axis=0, tiled=True)  17.7 us
    all_to_all x2, starting transfers between devices, sent_and_summed(): lax.all_to_all(tiles, axis, split_axis=0, concat_axis=0, tiled=True)  8.89 us
    unnamed x28, local copies, waits for them, and re-layouts  8.19 us
  transfers between devices with their start and end apart: 7, of which 6 were waited for; matrix products, arithmetic and copies ran while one was open for 6% of the time, Pallas kernels for 0%

profile of v1, /device:TPU:1, one launch (start us, length us, event | category | flops | bytes accessed | tf_op | source)
XLA Modules:
  0.0 232.5 jit_solution(15454773340022677375)
XLA Ops:
  2.1 1.1 reduce.19
  3.2 22.6 %all_to_all.45 = bf16[32,2,640]{2,1,0:T(2,128)(2,1)S(1)} all-to-all(bf16[32,2,640]{2,1,0:T(2,128)(2,1)S(1)} %reshape.1165), channel_id=1, replica_groups=mesh['seq_0'=8,'seq_1'=2,'exp_0'=4,'exp_1'=8] {'exp_0','exp_1'}, dimensions={0} | all-to-all | bytes 163840 | tf_op jit(solution)/shard_map/all_to_all | solution.py:27
  26.4 13.3 %all-gather.8 = f32[8,2,32]{2,1,0:T(2,128)S(1)} all-gather(f32[1,2,32]{2,1,0:T(2,128)S(1)} %maximum_bitcast_fusion.1), channel_id=2, replica_groups=mesh['seq_0'=8,'seq_1'=2,'exp_0'=4,'exp_1'=8] {'seq_0'}, dimensions={0}, use_global_device_ids=true | all-gather | bytes 2304 | tf_op jit(solution)/shard_map/all_gather | solution.py:52
  39.8 7.0 %all-gather.9 = f32[2,2,32]{2,1,0:T(2,128)S(1)} all-gather(f32[1,2,32]{2,1,0:T(2,128)S(1)} %maximum_bitcast_fusion.2), channel_id=3, replica_groups=mesh['seq_0'=8,'seq_1'=2,'exp_0'=4,'exp_1'=8] {'seq_1'}, dimensions={0}, use_global_device_ids=true | all-gather | bytes 768 | tf_op jit(solution)/shard_map/all_gather | solution.py:52
  46.8 6.1 %all-gather.10 = f32[4,2,32]{2,1,0:T(2,128)S(1)} all-gather(f32[1,2,32]{2,1,0:T(2,128)S(1)} %maximum_bitcast_fusion.3), channel_id=4, replica_groups=mesh['seq_0'=8,'seq_1'=2,'exp_0'=4,'exp_1'=8] {'exp_0'}, dimensions={0}, use_global_device_ids=true | all-gather | bytes 1280 | tf_op jit(solution)/shard_map/all_gather | solution.py:52
  53.0 10.5 %all-gather.11 = f32[8,2,32]{2,1,0:T(2,128)S(1)} all-gather(f32[1,2,32]{2,1,0:T(2,128)S(1)} %maximum_bitcast_fusion.4), channel_id=5, replica_groups=mesh['seq_0'=8,'seq_1'=2,'exp_0'=4,'exp_1'=8] {'exp_1'}, dimensions={0}, use_global_device_ids=true | all-gather | bytes 2304 | tf_op jit(solution)/shard_map/all_gather | solution.py:52
  65.0 4.5 %all-to-all-start.1 = ((f32[32,1,2560]{2,1,0:T(1,128)}), f32[32,1,2560]{2,1,0:T(1,128)S(1)}, u32[]{:S(2)}, u32[]{:S(2)}) async-start(f32[32,1,2560]{2,1,0:T(1,128)} %copy.17), calls=%async_computation.1 | async-start | bytes 655360 | tf_op jit(solution)/shard_map/all_to_all | solution.py:21
  69.6 9.9 %all-to-all-done.1 = f32[32,1,2560]{2,1,0:T(1,128)S(1)} async-done(((f32[32,1,2560]{2,1,0:T(1,128)}), f32[32,1,2560]{2,1,0:T(1,128)S(1)}, u32[]{:S(2)}, u32[]{:S(2)}) %all-to-all-start.1) | async-done | bytes 327712 | tf_op jit(solution)/shard_map/all_to_all | solution.py:21
  79.8 21.2 %all_to_all.46 = f32[16,1,2560]{2,1,0:T(1,128)S(1)} all-to-all(f32[16,1,2560]{2,1,0:T(1,128)S(1)} %broadcast_in_dim.15), channel_id=1, replica_groups=mesh['seq_0'=8,'seq_1'=2,'exp_0'=4,'exp_1'=8] {'seq_0','seq_1'}, dimensions={0} | all-to-all | bytes 327680 | tf_op jit(solution)/shard_map/all_to_all | solution.py:27
  102.7 3.4 %all-to-all-start.5 = ((f32[16,1,1280]{2,1,0:T(1,128)}), f32[16,1,1280]{2,1,0:T(1,128)S(1)}, u32[]{:S(2)}, u32[]{:S(2)}) async-start(f32[16,1,1280]{2,1,0:T(1,128)} %broadcast_in_dim.36), calls=%async_computation.5 | async-start | bytes 163840 | tf_op jit(solution)/shard_map/all_to_all | solution.py:27
  106.4 7.4 %all-to-all-done.5 = f32[16,1,1280]{2,1,0:T(1,128)S(1)} async-done(((f32[16,1,1280]{2,1,0:T(1,128)}), f32[16,1,1280]{2,1,0:T(1,128)S(1)}, u32[]{:S(2)}, u32[]{:S(2)}) %all-to-all-start.5) | async-done | bytes 81952 | tf_op jit(solution)/shard_map/all_to_all | solution.py:27
  114.5 3.4 %all-to-all-start.3 = ((f32[16,1,1280]{2,1,0:T(1,128)}), f32[16,1,1280]{2,1,0:T(1,128)S(1)}, u32[]{:S(2)}, u32[]{:S(2)}) async-start(f32[16,1,1280]{2,1,0:T(1,128)} %broadcast_in_dim.16), calls=%async_computation.3 | async-start | bytes 163840 | tf_op jit(solution)/shard_map/all_to_all | solution.py:27
  117.9 1.3 dynamic-slice.3
  119.2 1.3 dynamic-slice.2
  121.8 1.3 dynamic-slice.1
  123.7 1.3 dynamic-slice
  125.8 1.1 reduce.21
  127.6 4.8 %all-to-all-start.6 = ((bf16[32,2,640]{2,1,0:T(2,128)(2,1)}), bf16[32,2,640]{2,1,0:T(2,128)(2,1)S(1)}, u32[]{:S(2)}, u32[]{:S(2)}) async-start(bf16[32,2,640]{2,1,0:T(2,128)(2,1)} %reshape.1169), calls=%async_computation.6 | async-start | bytes 163840 | tf_op jit(solution)/shard_map/all_to_all | solution.py:27
  132.4 1.4 multiply_convert_fusion
  134.0 1.1 reduce.20
  135.8 5.6 %all-to-all-done.6 = bf16[32,2,640]{2,1,0:T(2,128)(2,1)S(1)} async-done(((bf16[32,2,640]{2,1,0:T(2,128)(2,1)}), bf16[32,2,640]{2,1,0:T(2,128)(2,1)S(1)}, u32[]{:S(2)}, u32[]{:S(2)}) %all-to-all-start.6) | async-done | bytes 81952 | tf_op jit(solution)/shard_map/all_to_all | solution.py:27
  141.4 3.9 %all-to-all-start.4 = ((bf16[32,2,640]{2,1,0:T(2,128)(2,1)}), bf16[32,2,640]{2,1,0:T(2,128)(2,1)S(1)}, u32[]{:S(2)}, u32[]{:S(2)}) async-start(bf16[32,2,640]{2,1,0:T(2,128)(2,1)} %reshape.1167), calls=%async_computation.4 | async-start | bytes 163840 | tf_op jit(solution)/shard_map/all_to_all | solution.py:27
  145.5 8.7 %all-to-all-done.4 = bf16[32,2,640]{2,1,0:T(2,128)(2,1)S(1)} async-done(((bf16[32,2,640]{2,1,0:T(2,128)(2,1)}), bf16[32,2,640]{2,1,0:T(2,128)(2,1)S(1)}, u32[]{:S(2)}, u32[]{:S(2)}) %all-to-all-start.4) | async-done | bytes 81952 | tf_op jit(solution)/shard_map/all_to_all | solution.py:27
  154.7 13.4 %all-reduce = f32[256]{0:T(256)S(1)} all-reduce(f32[256]{0:T(256)S(1)} %dynamic-update-slice), channel_id=6, replica_groups=mesh['seq_0'=8,'seq_1'=2,'exp_0'=4,'exp_1'=8] {'seq_0'}, use_global_device_ids=true, to_apply=%add | all-reduce | flops 256 | bytes 2048
  168.5 8.8 %all-reduce.1 = f32[64]{0:T(128)S(1)} all-reduce(f32[64]{0:T(128)S(1)} %dynamic-update-slice.1), channel_id=7, replica_groups=mesh['seq_0'=8,'seq_1'=2,'exp_0'=4,'exp_1'=8] {'seq_1'}, use_global_device_ids=true, to_apply=%add.1 | all-reduce | flops 64 | bytes 512
  177.6 6.8 %all-reduce.2 = f32[128]{0:T(128)S(1)} all-reduce(f32[128]{0:T(128)S(1)} %dynamic-update-slice.2), channel_id=8, replica_groups=mesh['seq_0'=8,'seq_1'=2,'exp_0'=4,'exp_1'=8] {'exp_0'}, use_global_device_ids=true, to_apply=%add.2 | all-reduce | flops 128 | bytes 1024
  184.8 11.3 %all-reduce.3 = f32[256]{0:T(256)S(1)} all-reduce(f32[256]{0:T(256)S(1)} %dynamic-update-slice.3), channel_id=9, replica_groups=mesh['seq_0'=8,'seq_1'=2,'exp_0'=4,'exp_1'=8] {'exp_1'}, use_global_device_ids=true, to_apply=%add.3 | all-reduce | flops 256 | bytes 2048
  197.3 4.4 %all-to-all-start.7 = ((f32[32,1,1280]{2,1,0:T(1,128)}), f32[32,1,1280]{2,1,0:T(1,128)S(1)}, u32[]{:S(2)}, u32[]{:S(2)}) async-start(f32[32,1,1280]{2,1,0:T(1,128)} %copy.21), calls=%async_computation.7 | async-start | bytes 327680 | tf_op jit(solution)/shard_map/all_to_all | solution.py:21
  202.0 1.1 fusion
  203.1 7.8 %all-to-all-done.7 = f32[32,1,1280]{2,1,0:T(1,128)S(1)} async-done(((f32[32,1,1280]{2,1,0:T(1,128)}), f32[32,1,1280]{2,1,0:T(1,128)S(1)}, u32[]{:S(2)}, u32[]{:S(2)}) %all-to-all-start.7) | async-done | bytes 163872 | tf_op jit(solution)/shard_map/all_to_all | solution.py:21
  211.7 12.1 %all-to-all-start.8 = ((f32[16,1,1280]{2,1,0:T(1,128)}), f32[16,1,1280]{2,1,0:T(1,128)S(1)}, u32[]{:S(2)}, u32[]{:S(2)}) async-start(f32[16,1,1280]{2,1,0:T(1,128)} %broadcast_in_dim.38), calls=%async_computation.8 | async-start | bytes 163840 | tf_op jit(solution)/shard_map/all_to_all | solution.py:27
  224.8 7.1 %all-to-all-done.8 = f32[16,1,1280]{2,1,0:T(1,128)S(1)} async-done(((f32[16,1,1280]{2,1,0:T(1,128)}), f32[16,1,1280]{2,1,0:T(1,128)S(1)}, u32[]{:S(2)}, u32[]{:S(2)}) %all-to-all-start.8) | async-done | bytes 81952 | tf_op jit(solution)/shard_map/all_to_all | solution.py:27
  (78 shorter events, 14.1 us)
Async XLA Ops:
  0.6 100.8 %copy-start = (bf16[1,320,1280]{2,1,0:T(8,128)(2,1)S(1)}, bf16[1,320,1280]{2,1,0:T(8,128)(2,1)}, u32[]{:S(2)}) copy-start(bf16[1,320,1280]{2,1,0:T(8,128)(2,1)} %param.7) | copy-start | bytes 2457604
  0.6 25.2 %copy-start.1 = (bf16[128,1280]{1,0:T(8,128)(2,1)S(1)}, bf16[128,1280]{1,0:T(8,128)(2,1)}, u32[]{:S(2)}) copy-start(bf16[128,1280]{1,0:T(8,128)(2,1)} %param.5) | copy-start | bytes 983044
  3.2 60.6 %copy-start.3 = (bf16[128,1280]{1,0:T(8,128)(2,1)S(1)}, bf16[128,1280]{1,0:T(8,128)(2,1)}, u32[]{:S(2)}) copy-start(bf16[128,1280]{1,0:T(8,128)(2,1)} %param.9) | copy-start | bytes 983044
  65.0 36.1 %copy-start.2 = (bf16[1,320,1280]{2,1,0:T(8,128)(2,1)S(1)}, bf16[1,320,1280]{2,1,0:T(8,128)(2,1)}, u32[]{:S(2)}) copy-start(bf16[1,320,1280]{2,1,0:T(8,128)(2,1)} %param.8) | copy-start | bytes 2457604
  65.0 14.4 %all-to-all-start.1 = ((f32[32,1,2560]{2,1,0:T(1,128)}), f32[32,1,2560]{2,1,0:T(1,128)S(1)}, u32[]{:S(2)}, u32[]{:S(2)}) async-start(f32[32,1,2560]{2,1,0:T(1,128)} %copy.17), calls=%async_computation.1 | async-start | bytes 655360 | tf_op jit(solution)/shard_map/all_to_all | solution.py:21
  102.7 11.1 %all-to-all-start.5 = ((f32[16,1,1280]{2,1,0:T(1,128)}), f32[16,1,1280]{2,1,0:T(1,128)S(1)}, u32[]{:S(2)}, u32[]{:S(2)}) async-start(f32[16,1,1280]{2,1,0:T(1,128)} %broadcast_in_dim.36), calls=%async_computation.5 | async-start | bytes 163840 | tf_op jit(solution)/shard_map/all_to_all | solution.py:27
  114.5 13.1 %all-to-all-start.3 = ((f32[16,1,1280]{2,1,0:T(1,128)}), f32[16,1,1280]{2,1,0:T(1,128)S(1)}, u32[]{:S(2)}, u32[]{:S(2)}) async-start(f32[16,1,1280]{2,1,0:T(1,128)} %broadcast_in_dim.16), calls=%async_computation.3 | async-start | bytes 163840 | tf_op jit(solution)/shard_map/all_to_all | solution.py:27
  127.6 13.8 %all-to-all-start.6 = ((bf16[32,2,640]{2,1,0:T(2,128)(2,1)}), bf16[32,2,640]{2,1,0:T(2,128)(2,1)S(1)}, u32[]{:S(2)}, u32[]{:S(2)}) async-start(bf16[32,2,640]{2,1,0:T(2,128)(2,1)} %reshape.1169), calls=%async_computation.6 | async-start | bytes 163840 | tf_op jit(solution)/shard_map/all_to_all | solution.py:27
  141.4 12.8 %all-to-all-start.4 = ((bf16[32,2,640]{2,1,0:T(2,128)(2,1)}), bf16[32,2,640]{2,1,0:T(2,128)(2,1)S(1)}, u32[]{:S(2)}, u32[]{:S(2)}) async-start(bf16[32,2,640]{2,1,0:T(2,128)(2,1)} %reshape.1167), calls=%async_computation.4 | async-start | bytes 163840 | tf_op jit(solution)/shard_map/all_to_all | solution.py:27
  197.3 13.6 %all-to-all-start.7 = ((f32[32,1,1280]{2,1,0:T(1,128)}), f32[32,1,1280]{2,1,0:T(1,128)S(1)}, u32[]{:S(2)}, u32[]{:S(2)}) async-start(f32[32,1,1280]{2,1,0:T(1,128)} %copy.21), calls=%async_computation.7 | async-start | bytes 327680 | tf_op jit(solution)/shard_map/all_to_all | solution.py:21
  211.7 20.2 %all-to-all-start.8 = ((f32[16,1,1280]{2,1,0:T(1,128)}), f32[16,1,1280]{2,1,0:T(1,128)S(1)}, u32[]{:S(2)}, u32[]{:S(2)}) async-start(f32[16,1,1280]{2,1,0:T(1,128)} %broadcast_in_dim.38), calls=%async_computation.8 | async-start | bytes 163840 | tf_op jit(solution)/shard_map/all_to_all | solution.py:27
